TPU v7x, 32 devices: a whole 2x2x4 slice. The times are simulated.
32 devices in a mesh: row: 4 (over y, core), col: 8 (over z, x).
Axes of the slice: x: 2, y: 2, z: 4, core: 2. Of those that a mesh axis runs over, the one named last changes fastest.
Arguments:
- excitons: float32 [1024, 1024], P('row', 'col'), may hold values from -500 to 500
- valence_energy: float32 [1024], P('row'), may hold values from -3 to -1
- conduction_energy: float32 [1024], P('col'), may hold values from 1 to 3
- psi_valence: float32 [4096, 1024], P('row', 'col'), may hold values from -0.1875 to 0.1875
- psi_conduction: float32 [4096, 1024], P('col', 'row'), may hold values from -0.1875 to 0.1875
- screened: float32 [4096, 4096], P('row', 'col'), may hold values from -0.9 to 0.975, as said below
Outputs:
- next_vector: float32 [1024, 1024], P('row', 'col')
- coefficients: float32 [4], replicated
Inputs may be any that keep to these rules, and one draw needn't show every extreme that they name: symmetric: screened[p, p'] = screened[p', p].
All inputs are finite; a program needn't handle non-finite values.
Results may differ from a plain program's by a relative error of at most 0.0003.
Values sent between devices are 32-bit elements; how exact they have to be, the bound alone decides.
A program may use at most 64 MiB of HBM per device.

v0:
```python
import jax
import jax.numpy as jnp
from jax import lax
from jax.sharding import PartitionSpec as P

NV = 1024
NC = 1024
STEPS = 2


EPS = 1e-06


def shards(excitons, valence_energy, conduction_energy, psi_valence, psi_conduction, screened):
    high = lax.Precision.HIGHEST
    count = NV * NC
    energy_gap = conduction_energy[None, :] - valence_energy[:, None]
    total = lax.psum(jnp.sum(excitons * excitons), ("row", "col"))
    vector = excitons / jnp.sqrt(total / count + EPS)
    previous = jnp.zeros_like(vector)
    beta_prev = jnp.zeros((), jnp.float32)
    values = []
    for step in range(STEPS):
        panel_valence = lax.all_gather(psi_valence, "col", axis=1, tiled=True)
        panel_conduction = lax.all_gather(psi_conduction, "row", axis=1, tiled=True)
        full_rows = lax.all_gather(vector, "col", axis=1, tiled=True)
        image_block = jnp.dot(full_rows, panel_conduction.T, precision=high)
        image_columns = lax.all_gather(image_block, "row", axis=0, tiled=True)
        points = jnp.dot(panel_valence, image_columns, precision=high)
        weighted = points * screened
        back_valence = lax.psum_scatter(
            jnp.dot(panel_valence.T, weighted, precision=high),
            "row",
            scatter_dimension=0,
            tiled=True,
        )
        back_flipped = back_valence.T
        kernel_flipped = lax.psum_scatter(
            jnp.dot(panel_conduction.T, back_flipped, precision=high),
            "col",
            scatter_dimension=0,
            tiled=True,
        )
        image = energy_gap * vector - kernel_flipped.T
        cross, square, older = lax.psum(
            (jnp.sum(vector * image), jnp.sum(image * image), jnp.sum(previous * image)),
            ("row", "col"),
        )
        alpha = cross / count
        residual = image - alpha * vector - beta_prev * previous
        squared = (
            square / count - alpha * alpha - 2.0 * beta_prev * older / count + beta_prev * beta_prev
        )
        beta = jnp.sqrt(squared + EPS)
        previous = vector
        vector = residual / beta
        beta_prev = beta
        values.append(alpha)
        values.append(beta)
    return (vector, jnp.stack(values))


def solution(mesh):
    return jax.shard_map(
        shards,
        mesh=mesh,
        in_specs=(
            P("row", "col"),
            P("row"),
            P("col"),
            P("row", "col"),
            P("col", "row"),
            P("row", "col"),
        ),
        out_specs=(P("row", "col"), P()),
        check_vma=False,
    )
```

profile of v0, /device:TPU:0, one launch (start us, length us, event | category | flops | bytes accessed | tf_op | source)
XLA Modules:
  0.0 619.4 jit_solution(2300817398218281370)
XLA Ops:
  7.2 0.0 all-gather.7.cloned.1.call-start
  7.2 1.5 multiply_reduce_fusion.6
  8.8 42.2 %psum.49 = f32[]{:T(128)} all-reduce(f32[]{:T(128)} %multiply_reduce_fusion.6), channel_id=1, replica_groups=mesh['row'=4,'col'=8] {'row','col'}, use_global_device_ids=true, to_apply=%region_1.0 | all-reduce | flops 1 | bytes 8 | tf_op jit(solution)/shard_map/psum | solution.py:18
  51.6 1.6 broadcast_divide_fusion
  53.2 0.0 all-gather.7.cloned.1.call-update
  53.2 0.0 all-gather.9.cloned.1.call-start
  53.3 0.7 all-gather.9.cloned.1.call-update
  54.0 0.0 all-gather.11.cloned.1.call-start
  54.0 38.7 %all-gather.7.cloned.1.call-done = f32[256,1024]{1,0:T(8,128)} async-done(((f32[256,128]{1,0:T(8,128)}), f32[256,1024]{1,0:T(8,128)}) %all-gather.7.cloned.1.call-update) | async-done | bytes 1048592 | tf_op jit(solution)/shard_map/all_gather | solution.py:26
  92.8 23.2 %all-gather.9.cloned.1.call-done = f32[512,1024]{1,0:T(8,128)} async-done(((f32[512,256]{1,0:T(8,128)}), f32[512,1024]{1,0:T(8,128)}) %all-gather.9.cloned.1.call-update) | async-done | bytes 2097168 | tf_op jit(solution)/shard_map/all_gather | solution.py:25
  115.9 4.7 fusion.6
  120.6 0.0 all-gather.11.cloned.1.call-update
  120.7 0.0 all-gather.13.cloned.1.call-start
  120.7 0.5 all-gather.13.cloned.1.call-update
  121.3 0.2 reduce-scatter.5.cloned.1.call-start
  121.5 21.9 %all-gather.11.cloned.1.call-done = f32[1024,512]{1,0:T(8,128)} async-done(((f32[256,512]{1,0:T(8,128)}), f32[1024,512]{1,0:T(8,128)}) %all-gather.11.cloned.1.call-update) | async-done | bytes 2097168 | tf_op jit(solution)/shard_map/all_gather | solution.py:28
  143.4 76.6 %all-gather.13.cloned.1.call-done = f32[1024,1024]{1,0:T(8,128)} async-done(((f32[1024,128]{1,0:T(8,128)}), f32[1024,1024]{1,0:T(8,128)}) %all-gather.13.cloned.1.call-update) | async-done | bytes 4194320 | tf_op jit(solution)/shard_map/all_gather | solution.py:24
  219.9 9.4 %fusion.7 = f32[512,1024]{0,1:T(8,128)S(1)} fusion(f32[1024,512]{1,0:T(8,128)} %all-gather.11.cloned.1.call-done, f32[1024,1024]{1,0:T(8,128)} %all-gather.13.cloned.1.call-done), kind=kOutput, calls=%fused_computation.24 | convolution fusion | flops 6442450944 | bytes 8388608 | tf_op jit(solution)/shard_map/dot_general | solution.py:29
  229.4 8.2 %fusion.2 = f32[1024,512]{0,1:T(8,128)} fusion(f32[1024,1024]{1,0:T(8,128)S(1)} %copy-done, f32[1024,512]{1,0:T(8,128)S(1)} %copy-done.3, f32[512,1024]{0,1:T(8,128)S(1)} %fusion.7), kind=kOutput, calls=%fused_computation.4 | convolution fusion | flops 6442975232 | bytes 10485760 | tf_op jit(solution)/shard_map/dot_general | solution.py:32
  237.7 0.0 reduce-scatter.5.cloned.1.call-update
  237.7 0.3 reduce-scatter.7.cloned.1.call-start
  238.0 29.2 %reduce-scatter.5.cloned.1.call-done = f32[256,512]{0,1:T(8,128)} async-done(((f32[1024,512]{0,1:T(8,128)}), f32[256,512]{0,1:T(8,128)}) %reduce-scatter.5.cloned.1.call-update) | async-done | bytes 524304 | tf_op jit(solution)/shard_map/reduce_scatter | solution.py:31
  267.2 3.9 convolution_bitcast_fusion.1
  271.1 0.0 reduce-scatter.7.cloned.1.call-update
  271.1 0.0 all-gather.15.cloned.1.call-start
  271.1 64.8 %reduce-scatter.7.cloned.1.call-done = f32[128,256]{0,1:T(8,128)} async-done(((f32[1024,256]{0,1:T(8,128)}), f32[128,256]{0,1:T(8,128)}) %reduce-scatter.7.cloned.1.call-update) | async-done | bytes 131088 | tf_op jit(solution)/shard_map/reduce_scatter | solution.py:38
  335.9 1.6 multiply_reduce_fusion.3
  337.5 40.1 %all-reduce.1 = (f32[]{:T(128)}, f32[]{:T(128)}, f32[]{:T(128)}) all-reduce(f32[]{:T(128)} %get-tuple-element.6, f32[]{:T(128)} %get-tuple-element.7, f32[]{:T(128)} %get-tuple-element.5), channel_id=1, replica_groups=mesh['row'=4,'col'=8] {'row','col'}, use_global_device_ids=true, to_apply=%region_7.0 | all-reduce | flops 3 | bytes 24 | tf_op jit(solution)/shard_map/psum | solution.py:45
  381.1 1.7 subtract_divide_fusion.1
  382.8 0.0 all-gather.15.cloned.1.call-update
  382.8 0.0 all-gather.17.cloned.1.call-start
  382.8 38.9 %all-gather.15.cloned.1.call-done = f32[256,1024]{1,0:T(8,128)} async-done(((f32[256,128]{1,0:T(8,128)}), f32[256,1024]{1,0:T(8,128)}) %all-gather.15.cloned.1.call-update) | async-done | bytes 1048592 | tf_op jit(solution)/shard_map/all_gather | solution.py:26
  421.7 4.0 fusion.8
  425.7 0.0 all-gather.17.cloned.1.call-update
  425.7 0.0 reduce-scatter.9.cloned.1.call-start
  425.8 21.7 %all-gather.17.cloned.1.call-done = f32[1024,512]{1,0:T(8,128)} async-done(((f32[256,512]{1,0:T(8,128)}), f32[1024,512]{1,0:T(8,128)}) %all-gather.17.cloned.1.call-update) | async-done | bytes 2097168 | tf_op jit(solution)/shard_map/all_gather | solution.py:28
  447.5 9.4 %fusion.9 = f32[512,1024]{0,1:T(8,128)S(1)} fusion(f32[1024,512]{1,0:T(8,128)} %all-gather.17.cloned.1.call-done, f32[1024,1024]{1,0:T(8,128)} %all-gather.13.cloned.1.call-done), kind=kOutput, calls=%fused_computation.26 | convolution fusion | flops 6442450944 | bytes 8388608 | tf_op jit(solution)/shard_map/dot_general | solution.py:29
  456.9 8.2 %fusion.3 = f32[1024,512]{0,1:T(8,128)} fusion(f32[1024,1024]{1,0:T(8,128)S(1)} %copy-done.1, f32[1024,512]{1,0:T(8,128)S(1)} %copy-done.4, f32[512,1024]{0,1:T(8,128)S(1)} %fusion.9), kind=kOutput, calls=%fused_computation.5 | convolution fusion | flops 6442975232 | bytes 10485760 | tf_op jit(solution)/shard_map/dot_general | solution.py:32
  465.2 0.0 reduce-scatter.9.cloned.1.call-update
  465.2 0.3 reduce-scatter.11.cloned.1.call-start
  465.5 31.0 %reduce-scatter.9.cloned.1.call-done = f32[256,512]{0,1:T(8,128)} async-done(((f32[1024,512]{0,1:T(8,128)}), f32[256,512]{0,1:T(8,128)}) %reduce-scatter.9.cloned.1.call-update) | async-done | bytes 524304 | tf_op jit(solution)/shard_map/reduce_scatter | solution.py:31
  496.5 3.9 convolution_bitcast_fusion
  500.4 0.0 reduce-scatter.11.cloned.1.call-update
  500.4 64.8 %reduce-scatter.11.cloned.1.call-done = f32[128,256]{0,1:T(8,128)} async-done(((f32[1024,256]{0,1:T(8,128)}), f32[128,256]{0,1:T(8,128)}) %reduce-scatter.11.cloned.1.call-update) | async-done | bytes 131088 | tf_op jit(solution)/shard_map/reduce_scatter | solution.py:38
  565.3 1.7 multiply_reduce_fusion
  566.9 40.1 %all-reduce = (f32[]{:T(128)}, f32[]{:T(128)}, f32[]{:T(128)}) all-reduce(f32[]{:T(128)} %get-tuple-element.3, f32[]{:T(128)} %get-tuple-element.4, f32[]{:T(128)} %get-tuple-element.2), channel_id=1, replica_groups=mesh['row'=4,'col'=8] {'row','col'}, use_global_device_ids=true, to_apply=%region_15.0 | all-reduce | flops 3 | bytes 24 | tf_op jit(solution)/shard_map/psum | solution.py:45
  610.3 0.6 pad_maximum_fusion
  610.9 1.7 subtract_divide_fusion
  (18 shorter events, 0.0 us)
Async XLA Ops:
  7.2 85.6 %all-gather.7.cloned.1.call-start = ((), (), s32[]{:S(2)}) async-start(), calls=%async_computation.4 | async-start | bytes 1179648 | tf_op jit(solution)/shard_map/all_gather | solution.py:26
  53.2 62.7 %all-gather.9.cloned.1.call-start = ((), (), s32[]{:S(2)}) async-start(), calls=%async_computation.5 | async-start | bytes 2621440 | tf_op jit(solution)/shard_map/all_gather | solution.py:25
  54.0 89.4 %all-gather.11.cloned.1.call-start = ((), (), s32[]{:S(2)}) async-start(), calls=%async_computation.6 | async-start | bytes 2621440 | tf_op jit(solution)/shard_map/all_gather | solution.py:28
  120.7 99.3 %all-gather.13.cloned.1.call-start = ((), (), s32[]{:S(2)}) async-start(), calls=%async_computation.7 | async-start | bytes 4718592 | tf_op jit(solution)/shard_map/all_gather | solution.py:24
  121.2 108.1 %copy-start.3 = (f32[1024,512]{1,0:T(8,128)S(1)}, f32[1024,512]{1,0:T(8,128)}, u32[]{:S(2)}) copy-start(f32[1024,512]{1,0:T(8,128)} %param.11) | copy-start | bytes 6291460
  121.3 145.9 %reduce-scatter.5.cloned.1.call-start = ((), (), s32[]{:S(2)}) async-start(), calls=%async_computation.8 | async-start | bytes 2621440 | tf_op jit(solution)/shard_map/reduce_scatter | solution.py:31
  219.9 9.4 %copy-start = (f32[1024,1024]{1,0:T(8,128)S(1)}, f32[1024,1024]{1,0:T(8,128)}, u32[]{:S(2)}) copy-start(f32[1024,1024]{1,0:T(8,128)} %all-gather.13.cloned.1.call-done) | copy-start | bytes 12582916
  237.7 29.5 %copy-start.2 = (f32[512,1024]{1,0:T(8,128)S(1)}, f32[512,1024]{1,0:T(8,128)}, u32[]{:S(2)}) copy-start(f32[512,1024]{1,0:T(8,128)} %all-gather.9.cloned.1.call-done) | copy-start | bytes 6291460
  237.7 98.2 %copy-start.5 = (f32[256,128]{1,0:T(8,128)S(1)}, f32[256,128]{1,0:T(8,128)}, u32[]{:S(2)}) copy-start(f32[256,128]{1,0:T(8,128)} %param.6) | copy-start | bytes 393220
  237.7 98.2 %copy-start.7 = (f32[256]{0:T(256)S(1)}, f32[256]{0:T(256)}, u32[]{:S(2)}) copy-start(f32[256]{0:T(256)} %param.7) | copy-start | bytes 3076
  237.7 98.2 %copy-start.8 = (f32[128]{0:T(128)S(1)}, f32[128]{0:T(128)}, u32[]{:S(2)}) copy-start(f32[128]{0:T(128)} %param.8) | copy-start | bytes 1540
  237.7 98.2 %reduce-scatter.7.cloned.1.call-start = ((), (), s32[]{:S(2)}) async-start(), calls=%async_computation.9 | async-start | bytes 1179648 | tf_op jit(solution)/shard_map/reduce_scatter | solution.py:38
  271.1 150.6 %all-gather.15.cloned.1.call-start = ((), (), s32[]{:S(2)}) async-start(), calls=%async_computation.10 | async-start | bytes 1179648 | tf_op jit(solution)/shard_map/all_gather | solution.py:26
  382.8 64.7 %all-gather.17.cloned.1.call-start = ((), (), s32[]{:S(2)}) async-start(), calls=%async_computation.11 | async-start | bytes 2621440 | tf_op jit(solution)/shard_map/all_gather | solution.py:28
  425.7 70.8 %reduce-scatter.9.cloned.1.call-start = ((), (), s32[]{:S(2)}) async-start(), calls=%async_computation.12 | async-start | bytes 2621440 | tf_op jit(solution)/shard_map/reduce_scatter | solution.py:31
  447.4 9.4 %copy-start.1 = (f32[1024,1024]{1,0:T(8,128)S(1)}, f32[1024,1024]{1,0:T(8,128)}, u32[]{:S(2)}) copy-start(f32[1024,1024]{1,0:T(8,128)} %all-gather.13.cloned.1.call-done) | copy-start | bytes 12582916
  447.5 9.4 %copy-start.4 = (f32[1024,512]{1,0:T(8,128)S(1)}, f32[1024,512]{1,0:T(8,128)}, u32[]{:S(2)}) copy-start(f32[1024,512]{1,0:T(8,128)} %param.11) | copy-start | bytes 6291460
  465.2 100.1 %copy-start.6 = (f32[256,128]{1,0:T(8,128)S(1)}, f32[256,128]{1,0:T(8,128)}, u32[]{:S(2)}) copy-start(f32[256,128]{1,0:T(8,128)} %subtract_divide_fusion.1) | copy-start | bytes 393220
  465.2 100.1 %reduce-scatter.11.cloned.1.call-start = ((), (), s32[]{:S(2)}) async-start(), calls=%async_computation.13 | async-start | bytes 1179648 | tf_op jit(solution)/shard_map/reduce_scatter | solution.py:38
Sparse Core Ops, SparseCore 0:
  53.3 39.3 all-gather.6
  94.3 21.5 all-gather.8
  120.8 22.5 all-gather.10
  145.3 74.6 all-gather.12
  237.8 29.3 reduce-scatter.4
  271.2 64.6 reduce-scatter.6
  382.9 38.7 all-gather.14
  425.8 21.5 all-gather.16
  465.3 31.1 reduce-scatter.8
  500.5 64.6 reduce-scatter.10
where the time goes:
time: 620 us; the launch traced here: 619 us
  waiting for transfers between devices  412 us (66%)
  blocking collectives  122 us (20%)
  matrix products  51.8 us (8%)
  between operations  21.6 us (3%)
  other arithmetic  10.3 us (2%)
    reduce_scatter x2, waiting for transfers between devices, shards(): lax.psum_scatter(jnp.dot(panel_conduction.T, back_flipped, precision=high...  130 us
    psum x2, blocking collectives, shards(): lax.psum((jnp.sum(vector * image), jnp.sum(image * image), jnp.sum(previo...  80.3 us
    all_gather x2, waiting for transfers between devices, shards(): full_rows = lax.all_gather(vector, 'col', axis=1, tiled=True)  77.6 us
    all_gather x1, waiting for transfers between devices, shards(): panel_valence = lax.all_gather(psi_valence, 'col', axis=1, tiled=True)  76.6 us
    reduce_scatter x2, waiting for transfers between devices, shards(): lax.psum_scatter(jnp.dot(panel_valence.T, weighted, precision=high), 'row...  60.2 us
    all_gather x2, waiting for transfers between devices, shards(): image_columns = lax.all_gather(image_block, 'row', axis=0, tiled=True)  43.6 us
    psum x1, blocking collectives, shards(): total = lax.psum(jnp.sum(excitons * excitons), ('row', 'col'))  42.2 us
    all_gather x1, waiting for transfers between devices, shards(): panel_conduction = lax.all_gather(psi_conduction, 'row', axis=1, tiled=True)  23.2 us
  transfers between devices with their start and end apart: 10, of which 10 were waited for; matrix products, arithmetic and copies ran while one was open for 0% of the time, Pallas kernels for 0%

commit v1 on v0

--- a/solution.py
+++ b/solution.py
@@ -1,6 +1,8 @@
 import jax
 import jax.numpy as jnp
 from jax import lax
+from jax.experimental import pallas as pl
+from jax.experimental.pallas import tpu as pltpu
 from jax.sharding import PartitionSpec as P
 
 NV = 1024
@@ -60,9 +62,322 @@
     return (vector, jnp.stack(values))
 
 
+MESH = pl.DeviceIdType.MESH
+NN = (((1,), (0,)), ((), ()))
+NT = (((1,), (1,)), ((), ()))
+
+
+def halves(value):
+    hi = value.astype(jnp.bfloat16)
+    return hi, (value - hi.astype(jnp.float32)).astype(jnp.bfloat16)
+
+
+def dot3(a, b, dims):
+    dot = lambda u, v: lax.dot_general(u, v, dims, preferred_element_type=jnp.float32)
+    return dot(a[0], b[0]) + (dot(a[0], b[1]) + dot(a[1], b[0]))
+
+
+def fused(
+    R, C, count,
+    x_ref, ve_ref, ce_ref, pv_ref, pc_ref, w_ref,
+    out_ref, coef_ref,
+    xl, pvl, pcl, il, cr, yr, xr, zr, bk, kb, sa, sb,
+    pv3, pc3, xs, im, wt, acc, wtr, q1, gap,
+    qz_s, qz_r, qx_s, qx_r, vz_s, vz_r, vx_s, vx_r,
+    cy_s, cy_r, cc_s, cc_r, iy_s, iy_r, ic_s, ic_r,
+    cr_s, cr_r, yr_s, yr_r, xr_s, xr_r, zr_s, zr_r,
+    sa_s, sa_r, sb_s, sb_r,
+):
+    NY, NZ = R // 2, C // 2
+    r, c = lax.axis_index("row"), lax.axis_index("col")
+    y, k, z, h = r // 2, r % 2, c // 2, c % 2
+    pending = []
+
+    def copy(src, dst, ss, rs, dev):
+        return pltpu.make_async_remote_copy(
+            src_ref=src, dst_ref=dst, send_sem=ss, recv_sem=rs, device_id=dev, device_id_type=MESH
+        )
+
+    def send(src, dst, ss, rs, dev):
+        op = copy(src, dst, ss, rs, dev)
+        op.start()
+        pending.append(op)
+
+    def wait(dst, ss, rs):
+        copy(dst, dst, ss, rs, (r, c)).wait_recv()
+
+    zdev = lambda d: (r, ((z + d) % NZ) * 2 + h)
+    zsrc = lambda d: ((z - d + NZ) % NZ) * 2 + h
+    xpeer = (r, z * 2 + 1 - h)
+    ydev = lambda d: (((y + d) % NY) * 2 + k, c)
+    ysrc = lambda d: ((y - d + NY) % NY) * 2 + k
+    kpeer = (y * 2 + 1 - k, c)
+    near = [d for d in range(1, NZ) if d in (1, NZ - 1)] + [d for d in range(2, NZ - 1)]
+
+    barrier = pltpu.get_barrier_semaphore()
+    for d in range(1, C):
+        pl.semaphore_signal(barrier, inc=1, device_id=(r, (c + d) % C), device_id_type=MESH)
+    for d in range(1, R):
+        pl.semaphore_signal(barrier, inc=1, device_id=((r + d) % R, c), device_id_type=MESH)
+    pl.semaphore_wait(barrier, C + R - 2)
+
+    def col_z(own, land, ss, rs):
+        for d in near:
+            send(own, land.at[c], ss.at[d], rs.at[d], zdev(d))
+
+    def col_own(own, land, ss, rs):
+        send(own, land.at[c], ss.at[0], rs.at[0], xpeer)
+
+    def col_forward(d, land, zs, zr_, ss, rs):
+        slot = land.at[zsrc(d)]
+        wait(slot, zs.at[d], zr_.at[d])
+        send(slot, slot, ss.at[d], rs.at[d], xpeer)
+
+    def col_done(d, land, ss, rs):
+        wait(land.at[((z - d + NZ) % NZ) * 2 + 1 - h], ss.at[d], rs.at[d])
+
+    def row_start(own, land, ys, yr_, cs, cr_):
+        for d in range(1, NY):
+            send(own, land.at[r], ys.at[d], yr_.at[d], ydev(d))
+        send(own, land.at[r], cs.at[0], cr_.at[0], kpeer)
+
+    def row_forward(d, land, ys, yr_, cs, cr_):
+        slot = land.at[ysrc(d)]
+        wait(slot, ys.at[d], yr_.at[d])
+        send(slot, slot, cs.at[d], cr_.at[d], kpeer)
+
+    def row_done(d, land, cs, cr_):
+        wait(land.at[((y - d + NY) % NY) * 2 + 1 - k], cs.at[d], cr_.at[d])
+
+    def reduce_start(i, values):
+        rows = [jnp.broadcast_to(v.reshape(1, 1), (1, 128)) for v in values]
+        rows += [jnp.zeros((1, 128), jnp.float32)] * (8 - len(rows))
+        sa[i, c] = jnp.concatenate(rows, axis=0)
+        for d in range(1, C):
+            send(sa.at[i, c], sa.at[i, c], sa_s.at[i, d], sa_r.at[i, d], (r, (c + d) % C))
+
+    def reduce_middle(i):
+        for d in range(1, C):
+            wait(sa.at[i, (c - d + C) % C], sa_s.at[i, d], sa_r.at[i, d])
+        sb[i, r] = jnp.sum(sa[i], axis=0)
+        for d in range(1, R):
+            send(sb.at[i, r], sb.at[i, r], sb_s.at[i, d], sb_r.at[i, d], ((r + d) % R, c))
+
+    def reduce_end(i):
+        for d in range(1, R):
+            wait(sb.at[i, (r - d + R) % R], sb_s.at[i, d], sb_r.at[i, d])
+        total = jnp.sum(sb[i], axis=0)
+        return [total[j : j + 1, :] for j in range(3)]
+
+    col_z(x_ref, xl.at[0], qz_s.at[0], qz_r.at[0])
+    col_own(x_ref, xl.at[0], qx_s.at[0], qx_r.at[0])
+    row_start(pc_ref, pcl, cy_s, cy_r, cc_s, cc_r)
+    col_z(pv_ref, pvl, vz_s, vz_r)
+    start = x_ref[...]
+    xl[0, c] = start
+    reduce_start(0, [jnp.sum(start * start)])
+    for d in near:
+        col_forward(d, xl.at[0], qz_s.at[0], qz_r.at[0], qx_s.at[0], qx_r.at[0])
+    col_own(pv_ref, pvl, vx_s, vx_r)
+    reduce_middle(0)
+    wtr[...] = w_ref[...].T
+    ve = jnp.broadcast_to(ve_ref[...], (ce_ref.shape[1], ve_ref.shape[1])).T
+    gap[...] = ce_ref[...] - ve
+    for d in range(1, NY):
+        row_forward(d, pcl, cy_s, cy_r, cc_s, cc_r)
+    ncl = x_ref.shape[1]
+
+    def split_pv(b, half):
+        hi, lo = halves(pvl[b] if half is None else half)
+        return hi, lo
+
+    def put_pv(block_z, block_h, value):
+        hi, lo = halves(value)
+        col = pl.ds(pl.multiple_of(block_h * ncl, 128), ncl)
+        pv3[0, block_z, :, col] = hi
+        pv3[1, block_z, :, col] = lo
+
+    def put_pc(block, value):
+        hi, lo = halves(value)
+        pc3[0, block] = hi
+        pc3[1, block] = lo
+
+    put_pc(r, pc_ref[...])
+    put_pv(z, h, pv_ref[...])
+    for d in range(NY):
+        row_done(d, pcl, cc_s, cc_r)
+    for d in range(1, R):
+        other = (r + d) % R
+        put_pc(other, pcl[other])
+    (total,) = reduce_end(0)[:1]
+    scale = 1.0 / jnp.sqrt(total / count + EPS)
+    q1[...] = start * scale
+    for d in range(NZ):
+        col_done(d, xl.at[0], qx_s.at[0], qx_r.at[0])
+
+    tile = 128
+    points = pc_ref.shape[0]
+    betas = None
+    for s in range(2):
+        for zz in range(NZ):
+            for hh in range(2):
+                b = zz * 2 + hh
+                if s == 0:
+                    value = xl[0, b] * scale
+                else:
+                    value = (xl[1, b] - alpha * (xl[0, b] * scale)) / beta
+                hi, lo = halves(value)
+                xs[0, zz, :, hh * ncl : (hh + 1) * ncl] = hi
+                xs[1, zz, :, hh * ncl : (hh + 1) * ncl] = lo
+        total = None
+        for zz in range(NZ):
+            part = dot3((pc3[0, zz], pc3[1, zz]), (xs[0, zz], xs[1, zz]), NT)
+            total = part if total is None else total + part
+        il[s, r] = total
+        row_start(il.at[s, r], il.at[s], iy_s.at[s], iy_r.at[s], ic_s.at[s], ic_r.at[s])
+        if s == 0:
+            for d in near:
+                col_forward(d, pvl, vz_s, vz_r, vx_s, vx_r)
+                put_pv((z - d + NZ) % NZ, h, pvl[zsrc(d)])
+                if d == near[0]:
+                    for e in range(1, NY):
+                        row_forward(e, il.at[s], iy_s.at[s], iy_r.at[s], ic_s.at[s], ic_r.at[s])
+            for d in [0] + near:
+                col_done(d, pvl, vx_s, vx_r)
+                zz = (z - d + NZ) % NZ
+                put_pv(zz, 1 - h, pvl[zz * 2 + 1 - h])
+
+        def chunk(b, first):
+            im[0], im[1] = halves(il[s, b])
+
+            def body(i, carry):
+                rows = pl.ds(pl.multiple_of(i * tile, tile), tile)
+                part = dot3((im[0, rows], im[1, rows]), (pv3[0, b], pv3[1, b]), NT)
+                acc[rows, :] = part if first else acc[rows, :] + part
+                return carry
+
+            lax.fori_loop(0, points // tile, body, 0)
+
+        chunk(r, True)
+        row_done(0, il.at[s], ic_s.at[s], ic_r.at[s])
+        chunk(y * 2 + 1 - k, False)
+        for e in range(1, NY):
+            if s == 1:
+                row_forward(e, il.at[s], iy_s.at[s], iy_r.at[s], ic_s.at[s], ic_r.at[s])
+            chunk(ysrc(e), False)
+            row_done(e, il.at[s], ic_s.at[s], ic_r.at[s])
+            chunk(((y - e + NY) % NY) * 2 + 1 - k, False)
+        wt[0], wt[1] = halves(acc[...] * wtr[...])
+
+        def back(b):
+            def body(i, carry):
+                rows = pl.ds(pl.multiple_of(i * tile, tile), tile)
+                bk[s, b, rows, :] = dot3((wt[0, rows], wt[1, rows]), (pv3[0, b], pv3[1, b]), NN)
+                return carry
+
+            lax.fori_loop(0, points // tile, body, 0)
+
+        for d in [*range(1, NY), 0]:
+            mine, theirs = ((y + d) % NY) * 2 + k, ((y + d) % NY) * 2 + 1 - k
+            back(theirs)
+            send(bk.at[s, theirs], cr.at[s, d], cr_s.at[s, d], cr_r.at[s, d], kpeer)
+            back(mine)
+            wait(cr.at[s, d], cr_s.at[s, d], cr_r.at[s, d])
+            bk[s, mine] = bk[s, mine] + cr[s, d]
+            if d > 0:
+                send(bk.at[s, mine], yr.at[s, d], yr_s.at[s, d], yr_r.at[s, d], ydev(d))
+        summed = bk[s, r]
+        for d in range(1, NY):
+            wait(yr.at[s, d], yr_s.at[s, d], yr_r.at[s, d])
+            summed = summed + yr[s, d]
+        flat = halves(summed.T)
+        far = [d for d in range(2, NZ - 1)] + [d for d in range(1, NZ) if d in (1, NZ - 1)] + [0]
+        for d in far:
+            zz = (z + d) % NZ
+            part = dot3(flat, (pc3[0, zz], pc3[1, zz]), NN)
+            kb[s, d, 0] = part[:, :ncl]
+            kb[s, d, 1] = part[:, ncl:]
+            send(kb.at[s, d, 1 - h], xr.at[s, d], xr_s.at[s, d], xr_r.at[s, d], xpeer)
+        for d in far:
+            wait(xr.at[s, d], xr_s.at[s, d], xr_r.at[s, d])
+            kb[s, d, h] = kb[s, d, h] + xr[s, d]
+            if d > 0:
+                send(kb.at[s, d, h], zr.at[s, d], zr_s.at[s, d], zr_r.at[s, d], zdev(d))
+        kernel = kb[s, 0, h]
+        for d in near:
+            wait(zr.at[s, d], zr_s.at[s, d], zr_r.at[s, d])
+            kernel = kernel + zr[s, d]
+        if s == 0:
+            vector = q1[...]
+            image = gap[...] * vector - kernel
+            xl[1, c] = image
+            col_z(xl.at[1, c], xl.at[1], qz_s.at[1], qz_r.at[1])
+            col_own(xl.at[1, c], xl.at[1], qx_s.at[1], qx_r.at[1])
+            reduce_start(1, [jnp.sum(vector * image), jnp.sum(image * image)])
+            reduce_middle(1)
+            for d in near:
+                col_forward(d, xl.at[1], qz_s.at[1], qz_r.at[1], qx_s.at[1], qx_r.at[1])
+            cross, square, _ = reduce_end(1)
+            alpha = cross / count
+            beta = jnp.sqrt(square / count - alpha * alpha + EPS)
+            coef_ref[0:1, :] = alpha
+            coef_ref[1:2, :] = beta
+            for d in range(NZ):
+                col_done(d, xl.at[1], qx_s.at[1], qx_r.at[1])
+        else:
+            vector = (xl[1, c] - alpha * q1[...]) / beta
+            previous = q1[...]
+            image = gap[...] * vector - kernel
+            reduce_start(2, [jnp.sum(vector * image), jnp.sum(image * image), jnp.sum(previous * image)])
+            reduce_middle(2)
+            cross, square, older = reduce_end(2)
+            alpha2 = cross / count
+            squared = square / count - alpha2 * alpha2 - 2.0 * beta * older / count + beta * beta
+            beta2 = jnp.sqrt(squared + EPS)
+            out_ref[...] = (image - alpha2 * vector - beta * previous) / beta2
+            coef_ref[2:3, :] = alpha2
+            coef_ref[3:4, :] = beta2
+    for op in pending:
+        op.wait_send()
+
+
+def fused_shards(R, C, excitons, valence_energy, conduction_energy, psi_valence, psi_conduction, screened):
+    nv, nc = excitons.shape
+    pr, pcn = screened.shape
+    f32, bf16 = jnp.float32, jnp.bfloat16
+    NY, NZ = R // 2, C // 2
+    vm, dma = pltpu.VMEM, pltpu.SemaphoreType.DMA
+    count = float(NV * NC)
+    scratch = [
+        vm((2, C, nv, nc), f32), vm((C, pr, nc), f32), vm((R, pcn, nv), f32), vm((2, R, pcn, nv), f32),
+        vm((2, NY, pcn, nv), f32), vm((2, NY, pcn, nv), f32),
+        vm((2, NZ, nv, nc), f32), vm((2, NZ, nv, nc), f32),
+        vm((2, R, pcn, nv), f32), vm((2, NZ, 2, nv, nc), f32),
+        vm((3, C, 8, 128), f32), vm((3, R, 8, 128), f32),
+        vm((2, R, pr, nv), bf16), vm((2, NZ, pcn, 2 * nc), bf16), vm((2, NZ, nv, 2 * nc), bf16),
+        vm((2, pcn, nv), bf16), vm((2, pcn, pr), bf16), vm((pcn, pr), f32), vm((pcn, pr), f32),
+        vm((nv, nc), f32), vm((nv, nc), f32),
+    ]
+    pairs = [(2, NZ), (2, NZ), (NZ,), (NZ,), (NY,), (NY,), (2, NY), (2, NY), (2, NY), (2, NY), (2, NZ), (2, NZ), (3, C), (3, R)]
+    for shape in pairs:
+        scratch += [dma(shape), dma(shape)]
+    vector, coef = pl.pallas_call(
+        lambda *refs: fused(R, C, count, *refs),
+        out_shape=(jax.ShapeDtypeStruct((nv, nc), f32), jax.ShapeDtypeStruct((4, 128), f32)),
+        in_specs=[pl.BlockSpec(memory_space=vm)] * 6,
+        out_specs=(pl.BlockSpec(memory_space=vm), pl.BlockSpec(memory_space=vm)),
+        scratch_shapes=scratch,
+        compiler_params=pltpu.CompilerParams(collective_id=0, has_side_effects=True, vmem_limit_bytes=67043328),
+    )(excitons, valence_energy.reshape(1, nv), conduction_energy.reshape(1, nc), psi_valence, psi_conduction, screened)
+    return vector, coef[:, 0]
+
+
 def solution(mesh):
+    R, C = mesh.shape["row"], mesh.shape["col"]
+    aligned = C == 2 * R and R % 2 == 0 and STEPS == 2 and NV == NC and (NV // R) % 128 == 0 and (NC // C) % 128 == 0
+    body = (lambda *args: fused_shards(R, C, *args)) if aligned else shards
     return jax.shard_map(
-        shards,
+        body,
         mesh=mesh,
         in_specs=(
             P("row", "col"),

time: 620 us -> 241 us (0.39)
  waiting for transfers between devices: 412 us -> 0 us
  Pallas kernels: 0 us -> 237 us
  blocking collectives: 122 us -> 0 us
  matrix products: 51.8 us -> 0 us
  between operations: 21.6 us -> 0.64 us
  other arithmetic: 10.3 us -> 0 us
    pallas_call x0 -> x1, Pallas kernels: none -> 237 us  [fused_shards(): pl.pallas_call(lambda *refs: fused(R, C, count, *refs), out_shape=(jax.Sh...]
    all_gather x6 -> x0, waiting for transfers between devices: 221 us -> none  [the longest x2 77.6 us: shards(): full_rows = lax.all_gather(vector, 'col', axis=1, tiled=True)]
    reduce_scatter x4 -> x0, waiting for transfers between devices: 190 us -> none  [the longest x2 130 us: shards(): lax.psum_scatter(jnp.dot(panel_conduction.T, back_flipped, precision=high...]
    psum x3 -> x0, blocking collectives: 122 us -> none  [the longest x2 80.3 us: shards(): lax.psum((jnp.sum(vector * image), jnp.sum(image * image), jnp.sum(previo...]
    dot_general x8 -> x0, matrix products: 51.8 us -> none  [the longest x2 18.9 us: shards(): points = jnp.dot(panel_valence, image_columns, precision=high)]
  transfers between devices with their start and end apart: 10 -> 0, of which waited for: 10 -> 0; matrix products, arithmetic and copies ran while one was open for 0% -> 0% of each run, Pallas kernels for 0% -> 0%
where the time goes in v1:
time: 241 us
  Pallas kernels  237 us (98%)
  local copies, waits for them, and re-layouts  2.86 us (1%)
    pallas_call x1, Pallas kernels, fused_shards(): pl.pallas_call(lambda *refs: fused(R, C, count, *refs), out_shape=(jax.Sh...  237 us

profile of v1, /device:TPU:0, one launch (start us, length us, event | category | flops | bytes accessed | tf_op | source)
XLA Modules:
  0.0 240.6 jit_solution(8918393355709416018)
XLA Ops:
  0.6 237.1 %shard_map.77 = (f32[256,128]{1,0:T(8,128)}, f32[4,128]{1,0:T(4,128)}) custom-call(f32[256,128]{1,0:T(8,128)} %refs_0_.1, f32[1,256]{1,0:T(1,128)} %bitcast.2, f32[1,128]{1,0:T(1,128)} %bitcast.3, f32[1024,128]{1,0:T(8,128)} %refs_3_.1, f32[512,256]{1,0:T(8,128)} %refs_4_.1, f32[1024,512]{1,0:T(8,128)} %refs_5_.1), custom_call_target="tpu_custom_call" | custom-call | tf_op jit(solution)/shard_map/pallas_call | solution.py:364
  237.8 1.3 slice_reduce_fusion
  239.1 1.6 copy.9

commit v2 on v1

--- a/solution.py
+++ b/solution.py
@@ -172,13 +172,17 @@
     col_z(x_ref, xl.at[0], qz_s.at[0], qz_r.at[0])
     col_own(x_ref, xl.at[0], qx_s.at[0], qx_r.at[0])
     row_start(pc_ref, pcl, cy_s, cy_r, cc_s, cc_r)
-    col_z(pv_ref, pvl, vz_s, vz_r)
+    half = pv_ref.shape[0] // 2
+    part_of = lambda j: pl.ds(j * half, half)
+    for j in range(2):
+        col_z(pv_ref.at[part_of(j)], pvl.at[j], vz_s.at[j], vz_r.at[j])
     start = x_ref[...]
     xl[0, c] = start
     reduce_start(0, [jnp.sum(start * start)])
     for d in near:
         col_forward(d, xl.at[0], qz_s.at[0], qz_r.at[0], qx_s.at[0], qx_r.at[0])
-    col_own(pv_ref, pvl, vx_s, vx_r)
+    for j in range(2):
+        col_own(pv_ref.at[part_of(j)], pvl.at[j], vx_s.at[j], vx_r.at[j])
     reduce_middle(0)
     wtr[...] = w_ref[...].T
     ve = jnp.broadcast_to(ve_ref[...], (ce_ref.shape[1], ve_ref.shape[1])).T
@@ -187,15 +191,11 @@
         row_forward(d, pcl, cy_s, cy_r, cc_s, cc_r)
     ncl = x_ref.shape[1]
 
-    def split_pv(b, half):
-        hi, lo = halves(pvl[b] if half is None else half)
-        return hi, lo
-
-    def put_pv(block_z, block_h, value):
+    def put_pv(j, block_z, block_h, value):
         hi, lo = halves(value)
         col = pl.ds(pl.multiple_of(block_h * ncl, 128), ncl)
-        pv3[0, block_z, :, col] = hi
-        pv3[1, block_z, :, col] = lo
+        pv3[0, block_z, part_of(j), col] = hi
+        pv3[1, block_z, part_of(j), col] = lo
 
     def put_pc(block, value):
         hi, lo = halves(value)
@@ -203,7 +203,8 @@
         pc3[1, block] = lo
 
     put_pc(r, pc_ref[...])
-    put_pv(z, h, pv_ref[...])
+    for j in range(2):
+        put_pv(j, z, h, pv_ref[part_of(j), :])
     for d in range(NY):
         row_done(d, pcl, cc_s, cc_r)
     for d in range(1, R):
@@ -215,8 +216,8 @@
     for d in range(NZ):
         col_done(d, xl.at[0], qx_s.at[0], qx_r.at[0])
 
-    tile = 128
     points = pc_ref.shape[0]
+    tile = points // 2
     betas = None
     for s in range(2):
         for zz in range(NZ):
@@ -237,15 +238,17 @@
         row_start(il.at[s, r], il.at[s], iy_s.at[s], iy_r.at[s], ic_s.at[s], ic_r.at[s])
         if s == 0:
             for d in near:
-                col_forward(d, pvl, vz_s, vz_r, vx_s, vx_r)
-                put_pv((z - d + NZ) % NZ, h, pvl[zsrc(d)])
+                for j in range(2):
+                    col_forward(d, pvl.at[j], vz_s.at[j], vz_r.at[j], vx_s.at[j], vx_r.at[j])
+                    put_pv(j, (z - d + NZ) % NZ, h, pvl[j, zsrc(d)])
                 if d == near[0]:
                     for e in range(1, NY):
                         row_forward(e, il.at[s], iy_s.at[s], iy_r.at[s], ic_s.at[s], ic_r.at[s])
             for d in [0] + near:
-                col_done(d, pvl, vx_s, vx_r)
-                zz = (z - d + NZ) % NZ
-                put_pv(zz, 1 - h, pvl[zz * 2 + 1 - h])
+                for j in range(2):
+                    col_done(d, pvl.at[j], vx_s.at[j], vx_r.at[j])
+                    zz = (z - d + NZ) % NZ
+                    put_pv(j, zz, 1 - h, pvl[j, zz * 2 + 1 - h])
 
         def chunk(b, first):
             im[0], im[1] = halves(il[s, b])
@@ -349,7 +352,7 @@
     vm, dma = pltpu.VMEM, pltpu.SemaphoreType.DMA
     count = float(NV * NC)
     scratch = [
-        vm((2, C, nv, nc), f32), vm((C, pr, nc), f32), vm((R, pcn, nv), f32), vm((2, R, pcn, nv), f32),
+        vm((2, C, nv, nc), f32), vm((2, C, pr // 2, nc), f32), vm((R, pcn, nv), f32), vm((2, R, pcn, nv), f32),
         vm((2, NY, pcn, nv), f32), vm((2, NY, pcn, nv), f32),
         vm((2, NZ, nv, nc), f32), vm((2, NZ, nv, nc), f32),
         vm((2, R, pcn, nv), f32), vm((2, NZ, 2, nv, nc), f32),
@@ -358,7 +361,7 @@
         vm((2, pcn, nv), bf16), vm((2, pcn, pr), bf16), vm((pcn, pr), f32), vm((pcn, pr), f32),
         vm((nv, nc), f32), vm((nv, nc), f32),
     ]
-    pairs = [(2, NZ), (2, NZ), (NZ,), (NZ,), (NY,), (NY,), (2, NY), (2, NY), (2, NY), (2, NY), (2, NZ), (2, NZ), (3, C), (3, R)]
+    pairs = [(2, NZ), (2, NZ), (2, NZ), (2, NZ), (NY,), (NY,), (2, NY), (2, NY), (2, NY), (2, NY), (2, NZ), (2, NZ), (3, C), (3, R)]
     for shape in pairs:
         scratch += [dma(shape), dma(shape)]
     vector, coef = pl.pallas_call(

time: 241 us -> 232 us (0.963)
  Pallas kernels: 237 us -> 228 us
    pallas_call x1, Pallas kernels: 237 us -> 228 us  [fused_shards(): pl.pallas_call(lambda *refs: fused(R, C, count, *refs), out_shape=(jax.Sh...]
where the time goes in v2:
time: 232 us
  Pallas kernels  228 us (98%)
  local copies, waits for them, and re-layouts  2.86 us (1%)
    pallas_call x1, Pallas kernels, fused_shards(): pl.pallas_call(lambda *refs: fused(R, C, count, *refs), out_shape=(jax.Sh...  228 us

profile of v2, /device:TPU:0, one launch (start us, length us, event | category | flops | bytes accessed | tf_op | source)
XLA Modules:
  0.0 231.8 jit_solution(16141667440523974713)
XLA Ops:
  0.6 228.3 %shard_map.77 = (f32[256,128]{1,0:T(8,128)}, f32[4,128]{1,0:T(4,128)}) custom-call(f32[256,128]{1,0:T(8,128)} %refs_0_.1, f32[1,256]{1,0:T(1,128)} %bitcast.2, f32[1,128]{1,0:T(1,128)} %bitcast.3, f32[1024,128]{1,0:T(8,128)} %refs_3_.1, f32[512,256]{1,0:T(8,128)} %refs_4_.1, f32[1024,512]{1,0:T(8,128)} %refs_5_.1), custom_call_target="tpu_custom_call" | custom-call | tf_op jit(solution)/shard_map/pallas_call | solution.py:367
  229.0 1.3 slice_reduce_fusion
  230.3 1.6 copy.9
